TPU v7x, 32 devices: a whole 2x2x4 slice. The times are simulated.
32 devices in a mesh: ctx: 8 (over y, x, core), head: 4 (over z).
Axes of the slice: x: 2, y: 2, z: 4, core: 2. Of those that a mesh axis runs over, the one named last changes fastest.
Arguments:
- prefix: bfloat16 [65536, 1024], P(('ctx', 'head')), may hold values from -6 to 6
- keep_blocks: int32 [4, 8, 16], P('head', 'ctx'), may hold values from 0 to 15, each once within a row
- keep_count: int32 [4, 8], P('head', 'ctx'), may hold values from 1 to 16, 64 in all within a row
- latent_inputs: bfloat16 [128, 1024], P('ctx'), may hold values from -6 to 6
- latent_pos: int32 [128], replicated, may hold values from 0 to 65535
- w_query: bfloat16 [1024, 1024], P(None, 'head')
- w_key: bfloat16 [1024, 1024], replicated, may hold values from -0.1875 to 0.1875
- w_value: bfloat16 [1024, 1024], replicated, may hold values from -0.1875 to 0.1875
Outputs:
- attended: bfloat16 [128, 1024], P('ctx', 'head')
Inputs may be any that keep to these rules, and one draw needn't show every extreme that they name: keep_blocks[h, c, :] lists each of the 16 block numbers once; the first keep_count[h, c] entries are the kept blocks. For every index h, keep_count[h, :] sums to 64, and its largest entry is 16.
All inputs are finite; a program needn't handle non-finite values. No bound on the sum of `keep_count` on one device may be relied on, other than what follows from the above.
Results may differ from a plain program's by a relative error of at most 0.0085.
The roundings to bfloat16 on the way count: a program that leaves them out, or rounds other values in their place, can miss the bound.
Values may be sent and summed in bfloat16 or wider, within the bound.
No kernel may reach another device: no remote copies, remote signals or barrier semaphores. Data moves between devices by JAX's collectives and lax.ppermute only.
A program may use at most 128 MiB of HBM per device.

v0:
```python
import jax
import jax.numpy as jnp
from jax import lax
from jax.sharding import PartitionSpec as P

HD = 64
BLOCK = 128


NEG_FILL = -1e30
EPSILON = 1e-06
QUERY_ROWS = 1024


def combined_all(array, axis, combine):
    everything = jax.tree.map(lambda part: lax.all_gather(part, axis), array)
    initial = jax.tree.map(lambda part: part[0], everything)

    def turn(k, so_far):
        return combine(so_far, jax.tree.map(lambda part: part[k], everything))

    return lax.fori_loop(1, lax.axis_size(axis), turn, initial)


def normalize(source_rows):
    wide_rows = source_rows.astype(jnp.float32)
    factor = lax.rsqrt(jnp.mean(wide_rows * wide_rows, axis=-1, keepdims=True) + EPSILON)
    return (wide_rows * factor).astype(jnp.bfloat16)


def widen(per_head):
    return jnp.repeat(per_head, HD, axis=1)


def join_partials(first, second):
    first_top, first_sums, first_weighted = first
    second_top, second_sums, second_weighted = second
    joined_top = jnp.maximum(first_top, second_top)
    first_scale = jnp.exp(first_top - joined_top)
    second_scale = jnp.exp(second_top - joined_top)
    joined_sums = first_sums * first_scale + second_sums * second_scale
    joined_weighted = first_weighted * widen(first_scale) + second_weighted * widen(second_scale)
    return (joined_top, joined_sums, joined_weighted)


def local_partials(queries, key_rows, value_rows, key_pos, key_valid, query_pos):
    key_count = key_rows.shape[0]
    heads_here = queries.shape[1] // HD
    latents = queries.shape[0]
    block_rows = min(QUERY_ROWS, latents)
    block_count = latents // block_rows
    key_heads = key_rows.reshape(key_count, heads_here, HD).transpose(1, 0, 2)
    value_heads = value_rows.reshape(key_count, heads_here, HD).transpose(1, 0, 2)
    query_heads = queries.reshape(block_count, block_rows, heads_here, HD).transpose(2, 0, 1, 3)
    pos_blocks = query_pos.reshape(block_count, block_rows)

    def per_head(head_args):
        key_head, value_head, query_head = head_args

        def per_block(block_args):
            query_block, pos_block = block_args
            scores = jnp.einsum(
                "qd,kd->qk", query_block, key_head, preferred_element_type=jnp.float32
            )
            allowed = key_valid[None, :] & (key_pos[None, :] < pos_block[:, None])
            masked = jnp.where(allowed, scores, NEG_FILL)
            row_top = jnp.max(masked, axis=1)
            weights = jnp.where(allowed, jnp.exp(masked - row_top[:, None]), 0.0)
            weight_sum = jnp.sum(weights, axis=1)
            weighted = jnp.dot(
                weights.astype(jnp.bfloat16), value_head, preferred_element_type=jnp.float32
            )
            return (row_top, weight_sum, weighted)

        return lax.map(per_block, (query_head, pos_blocks))

    row_tops, row_sums, weighted = lax.map(per_head, (key_heads, value_heads, query_heads))
    row_tops = row_tops.transpose(1, 2, 0).reshape(latents, heads_here)
    row_sums = row_sums.transpose(1, 2, 0).reshape(latents, heads_here)
    weighted = weighted.transpose(1, 2, 0, 3).reshape(latents, heads_here * HD)
    return (row_tops, row_sums, weighted)


def per_device(prefix, keep_blocks, keep_count, latent_inputs, latent_pos, w_query, w_key, w_value):
    head_count = lax.axis_size("head")
    ctx_index = lax.axis_index("ctx")
    head_index = lax.axis_index("head")
    block_total = keep_blocks.shape[2]
    head_width = w_query.shape[1]
    own_list = keep_blocks.reshape(1, block_total)
    own_count = keep_count.reshape(1)
    block_range = jnp.arange(block_total, dtype=jnp.int32)
    head_range = jnp.arange(head_count, dtype=jnp.int32)
    normed = normalize(prefix)
    row_count = prefix.shape[0]
    key_local = jnp.dot(normed, w_key, preferred_element_type=jnp.float32).astype(jnp.bfloat16)
    value_local = jnp.dot(normed, w_value, preferred_element_type=jnp.float32).astype(jnp.bfloat16)
    latent_normed = normalize(latent_inputs)
    latent_rows = latent_inputs.shape[0]
    heads_here = head_width // HD
    query_local = (
        jnp.dot(latent_normed, w_query, preferred_element_type=jnp.float32) * HD ** (-0.5)
    ).astype(jnp.bfloat16)
    own_key_cols = lax.dynamic_slice_in_dim(w_key, head_index * head_width, head_width, 1)
    own_value_cols = lax.dynamic_slice_in_dim(w_value, head_index * head_width, head_width, 1)
    self_key = jnp.dot(latent_normed, own_key_cols, preferred_element_type=jnp.float32).astype(
        jnp.bfloat16
    )
    self_value = jnp.dot(latent_normed, own_value_cols, preferred_element_type=jnp.float32).astype(
        jnp.bfloat16
    )
    self_score = jnp.sum(
        (query_local.astype(jnp.float32) * self_key.astype(jnp.float32)).reshape(
            latent_rows, heads_here, HD
        ),
        axis=2,
    )
    all_queries = lax.all_gather(query_local, "ctx", axis=0, tiled=True)
    own_first = ctx_index * latent_rows
    group_list, group_count = (
        lax.all_gather(own_list, "head", axis=0, tiled=True),
        lax.all_gather(own_count, "head", axis=0, tiled=True),
    )
    group_match = (group_list[:, :, None] == block_range[None, None, :]) & (
        block_range[None, :, None] < group_count[:, None, None]
    )
    valid_grid = jnp.repeat(jnp.any(group_match, axis=1), BLOCK, axis=1)
    shard_number = ctx_index * head_count + head_range
    pos_grid = (
        shard_number[:, None] * (block_total * BLOCK)
        + jnp.arange(block_total * BLOCK, dtype=jnp.int32)[None, :]
    )
    key_pos = pos_grid.reshape(-1)
    key_valid = valid_grid.reshape(-1)
    key_parts, value_parts = (
        lax.all_to_all(
            key_local.reshape(row_count, head_count, head_width),
            "head",
            split_axis=1,
            concat_axis=0,
            tiled=True,
        ),
        lax.all_to_all(
            value_local.reshape(row_count, head_count, head_width),
            "head",
            split_axis=1,
            concat_axis=0,
            tiled=True,
        ),
    )
    key_rows = key_parts.reshape(head_count * row_count, head_width)
    value_rows = value_parts.reshape(head_count * row_count, head_width)
    row_tops, row_sums, weighted = local_partials(
        all_queries, key_rows, value_rows, key_pos, key_valid, latent_pos
    )
    merged_top, merged_sums, merged_weighted = combined_all(
        (row_tops, row_sums, weighted), "ctx", join_partials
    )
    own_top = lax.dynamic_slice_in_dim(merged_top, own_first, latent_rows, 0)
    own_sums = lax.dynamic_slice_in_dim(merged_sums, own_first, latent_rows, 0)
    own_weighted = lax.dynamic_slice_in_dim(merged_weighted, own_first, latent_rows, 0)
    final_top = jnp.maximum(own_top, self_score)
    keep_scale = jnp.exp(own_top - final_top)
    self_weight = jnp.exp(self_score - final_top)
    denominator = own_sums * keep_scale + self_weight
    numerator = own_weighted * widen(keep_scale) + widen(self_weight) * self_value.astype(
        jnp.float32
    )
    return (numerator / widen(denominator)).astype(jnp.bfloat16)


def solution(mesh):
    return jax.shard_map(
        per_device,
        mesh=mesh,
        in_specs=(
            P(("ctx", "head"), None),
            P("head", "ctx", None),
            P("head", "ctx"),
            P("ctx", None),
            P(),
            P(None, "head"),
            P(),
            P(),
        ),
        out_specs=P("ctx", "head"),
        check_vma=False,
    )
```

profile of v0, /device:TPU:1, one launch (start us, length us, event | category | flops | bytes accessed | tf_op | source)
XLA Modules:
  0.0 330.9 jit_solution(14026656967225993386)
XLA Ops:
  6.5 3.2 fusion.26
  9.8 0.8 copy-done.1
  10.6 6.6 %convolution_convert_fusion.1 = bf16[2048,1024]{0,1:T(8,128)(2,1)} fusion(bf16[1024,1024]{1,0:T(8,128)(2,1)S(1)} %copy-done, bf16[2048,1024]{1,0:T(8,128)(2,1)S(1)} %copy-done.1, f32[2048]{0:T(1024)S(1)} %add_rsqrt_fusion), kind=kOutput, calls=%fused_computation.37 | convolution fusion | flops 4303355904 | bytes 10493952 | tf_op jit(solution)/shard_map/dot_general | solution.py:96
  17.2 5.4 %all-to-all-start = ((bf16[2048,4,256]{0,2,1:T(8,128)(2,1)}), bf16[2048,4,256]{0,2,1:T(8,128)(2,1)}, u32[]{:S(2)}, u32[]{:S(2)}) async-start(bf16[2048,4,256]{0,2,1:T(8,128)(2,1)} %bitcast.124), calls=%async_computation | async-start | bytes 8388608 | tf_op jit(solution)/shard_map/all_to_all | solution.py:136
  22.6 9.6 %convolution_convert_fusion = bf16[2048,1024]{0,1:T(8,128)(2,1)} fusion(bf16[1024,1024]{1,0:T(8,128)(2,1)} %param.19, bf16[2048,1024]{1,0:T(8,128)(2,1)} %param.12, f32[2048]{0:T(1024)S(1)} %add_rsqrt_fusion), kind=kOutput, calls=%fused_computation.36 | convolution fusion | flops 4303355904 | bytes 10493952 | tf_op jit(solution)/shard_map/dot_general | solution.py:97
  32.3 83.3 %all-to-all-done = bf16[2048,4,256]{0,2,1:T(8,128)(2,1)} async-done(((bf16[2048,4,256]{0,2,1:T(8,128)(2,1)}), bf16[2048,4,256]{0,2,1:T(8,128)(2,1)}, u32[]{:S(2)}, u32[]{:S(2)}) %all-to-all-start) | async-done | bytes 4194336 | tf_op jit(solution)/shard_map/all_to_all | solution.py:136
  115.5 5.0 %all-to-all-start.1 = ((bf16[2048,4,256]{0,2,1:T(8,128)(2,1)}), bf16[2048,4,256]{0,2,1:T(8,128)(2,1)}, u32[]{:S(2)}, u32[]{:S(2)}) async-start(bf16[2048,4,256]{0,2,1:T(8,128)(2,1)} %bitcast.122), calls=%async_computation.1 | async-start | bytes 8388608 | tf_op jit(solution)/shard_map/all_to_all | solution.py:143
  121.2 0.6 dynamic-slice
  121.8 0.7 bitcast_dynamic-update-slice_fusion
  122.5 91.0 %all-reduce = s32[4]{0:T(128)S(1)} all-reduce(s32[4]{0:T(128)S(1)} %bitcast_dynamic-update-slice_fusion), channel_id=3, replica_groups=mesh['ctx'=8,'head'=4] {'head'}, use_global_device_ids=true, to_apply=%add | all-reduce | flops 4 | bytes 32
  213.5 0.1 fusion.40
  213.6 0.2 fusion.30
  213.8 10.5 %all_gather.20 = bf16[128,256]{1,0:T(8,128)(2,1)S(1)} all-gather(bf16[16,256]{1,0:T(8,128)(2,1)S(1)} %fusion.30), channel_id=1, replica_groups=mesh['ctx'=8,'head'=4] {'ctx'}, dimensions={0}, use_global_device_ids=true | all-gather | bytes 73728 | tf_op jit(solution)/shard_map/all_gather | solution.py:118
  224.4 0.1 copy.59
  224.5 7.2 %all-gather = s32[4,1,16]{2,1,0:T(1,128)S(1)} all-gather(s32[1,1,16]{2,1,0:T(1,128)S(1)} %copy-done.5), channel_id=2, replica_groups=mesh['ctx'=8,'head'=4] {'head'}, dimensions={0}, use_global_device_ids=true | all-gather | bytes 320 | tf_op jit(solution)/shard_map/all_gather | solution.py:121
  231.7 0.1 fusion.43
  231.8 7.4 %copy.60 = bf16[4,2048,1,256]{1,0,3,2:T(4,128)(2,1)} copy(bf16[4,2048,1,256]{1,3,0,2:T(8,128)(2,1)} %bitcast.10) | data formatting | bytes 8388608 | tf_op jit(solution)/shard_map/all_to_all | solution.py:136
  239.2 7.8 %reshape_reshape.6 = bf16[8192,4,64]{0,2,1:T(8,128)(2,1)} reshape(bf16[4,2048,1,256]{1,0,3,2:T(4,128)(2,1)} %copy.60) | data formatting | bytes 8388608 | tf_op jit(solution)/shard_map/reshape;reshape | solution.py:52
  247.0 7.4 %copy.61 = bf16[4,2048,1,256]{1,0,3,2:T(4,128)(2,1)} copy(bf16[4,2048,1,256]{1,3,0,2:T(8,128)(2,1)} %bitcast.14) | data formatting | bytes 8388608 | tf_op jit(solution)/shard_map/all_to_all | solution.py:143
  254.4 7.8 %reshape_reshape.7 = bf16[8192,4,64]{0,2,1:T(8,128)(2,1)} reshape(bf16[4,2048,1,256]{1,0,3,2:T(4,128)(2,1)} %copy.61) | data formatting | bytes 8388608 | tf_op jit(solution)/shard_map/reshape;reshape | solution.py:53
  262.2 26.9 %while.41 = (s32[]{:T(128)}, f32[4,1,128]{2,1,0:T(1,128)S(1)}, f32[4,1,128]{2,1,0:T(1,128)S(1)}, f32[4,1,128,64]{2,3,1,0:T(8,128)S(1)}, s32[1,128]{1,0:T(1,128)S...) while((s32[]{:T(128)}, f32[4,1,128]{2,1,0:T(1,128)S(1)}, ...), condition=%wide.region_6.7_spmd.clone, body=%wide.region_3.6_spmd.clone.sunk | while | flops 283123456 | bytes 14966465 | solution.py:77
  262.3 2.5 fusion.69
  264.8 2.6 fusion.71
  267.5 1.4 fusion.70
  269.1 2.5 fusion.69
  271.6 2.6 fusion.71
  274.2 1.4 fusion.70
  275.8 2.5 fusion.69
  278.3 2.6 fusion.71
  280.9 1.4 fusion.70
  282.5 2.5 fusion.69
  285.0 2.6 fusion.71
  287.6 1.4 fusion.70
  289.0 0.7 copy.68
  289.8 0.2 fusion.37
  290.0 0.1 reshape.115
  290.1 0.1 reduce_sum.39
  290.2 10.9 %all_gather.22 = f32[8,128,4]{1,2,0:T(4,128)S(1)} all-gather(f32[1,128,4]{1,2,0:T(4,128)S(1)} %bitcast.136), channel_id=1, replica_groups=mesh['ctx'=8,'head'=4] {'ctx'}, dimensions={0}, use_global_device_ids=true | all-gather | bytes 18432 | tf_op jit(solution)/shard_map/all_gather | solution.py:16
  301.2 7.9 %all_gather.21 = f32[8,128,4]{1,2,0:T(4,128)S(1)} all-gather(f32[1,128,4]{1,2,0:T(4,128)S(1)} %bitcast.135), channel_id=1, replica_groups=mesh['ctx'=8,'head'=4] {'ctx'}, dimensions={0}, use_global_device_ids=true | all-gather | bytes 18432 | tf_op jit(solution)/shard_map/all_gather | solution.py:16
  309.1 3.4 %all-gather.4.cloned.1.call-done = f32[8,128,256]{2,1,0:T(8,128)} async-done(((f32[1,128,256]{2,1,0:T(8,128)}), f32[8,128,256]{2,1,0:T(8,128)}) %all-gather.4.cloned.1.call-update) | async-done | bytes 1048592 | tf_op jit(solution)/shard_map/all_gather | solution.py:16
  312.5 0.9 slice_bitcast_fusion
  313.4 0.1 copy.69
  313.5 7.8 %while.40 = (s32[]{:T(128)}, f32[128,4]{0,1:T(4,128)S(1)}, f32[128,4]{0,1:T(4,128)S(1)}, f32[128,256]{0,1:T(8,128)S(1)}, f32[8,128,4]{1,2,0:T(4,128)S(1)}, /*ind...) while((s32[]{:T(128)}, f32[128,4]{0,1:T(4,128)S(1)}, ...), condition=%wide.region_8.9_spmd, body=%wide.region_7.8_spmd.sunk | while | flops 101381 | bytes 938135 | solution.py:22
  313.6 0.9 constant_dynamic-slice_fusion.2
  314.5 0.1 copy.81
  314.7 0.9 constant_dynamic-slice_fusion.2
  315.6 0.1 copy.81
  315.8 0.9 constant_dynamic-slice_fusion.2
  316.7 0.1 copy.81
  316.9 0.9 constant_dynamic-slice_fusion.2
  317.8 0.1 copy.81
  318.0 0.9 constant_dynamic-slice_fusion.2
  318.9 0.1 copy.81
  319.1 0.9 constant_dynamic-slice_fusion.2
  320.1 0.1 copy.81
  320.3 0.9 constant_dynamic-slice_fusion.2
  321.2 0.1 copy.81
  321.3 0.1 copy.72
  321.5 0.1 copy.73
  321.7 0.1 reshape.116
  321.8 0.1 reshape.117
  322.0 0.1 reshape.118
  322.1 0.1 copy.71
  322.2 1.9 fusion.35
  (60 shorter events, 1.6 us)
Async XLA Ops:
  6.5 3.2 copy-start
  6.5 4.1 %copy-start.1 = (bf16[2048,1024]{1,0:T(8,128)(2,1)S(1)}, bf16[2048,1024]{1,0:T(8,128)(2,1)}, u32[]{:S(2)}) copy-start(bf16[2048,1024]{1,0:T(8,128)(2,1)} %param.12) | copy-start | bytes 12582916
  17.2 98.3 %all-to-all-start = ((bf16[2048,4,256]{0,2,1:T(8,128)(2,1)}), bf16[2048,4,256]{0,2,1:T(8,128)(2,1)}, u32[]{:S(2)}, u32[]{:S(2)}) async-start(bf16[2048,4,256]{0,2,1:T(8,128)(2,1)} %bitcast.124), calls=%async_computation | async-start | bytes 8388608 | tf_op jit(solution)/shard_map/all_to_all | solution.py:136
  115.5 5.7 %copy-start.6 = (u32[32]{0:T(128)S(1)}, u32[32]{0:T(128)}, u32[]{:S(2)}) copy-start(u32[32]{0:T(128)} %constant.119) | copy-start | bytes 388
  115.5 97.9 %copy-start.2 = (bf16[16,1024]{1,0:T(8,128)(2,1)S(1)}, bf16[16,1024]{1,0:T(8,128)(2,1)}, u32[]{:S(2)}) copy-start(bf16[16,1024]{1,0:T(8,128)(2,1)} %param.15) | copy-start | bytes 98308
  115.5 98.1 %copy-start.3 = (bf16[1024,256]{1,0:T(8,128)(2,1)S(1)}, bf16[1024,256]{1,0:T(8,128)(2,1)}, u32[]{:S(2)}) copy-start(bf16[1024,256]{1,0:T(8,128)(2,1)} %param.17) | copy-start | bytes 1572868
  115.5 108.9 %copy-start.5 = (s32[1,1,16]{2,1,0:T(1,128)S(1)}, s32[1,1,16]{2,1,0:T(1,128)}, u32[]{:S(2)}) copy-start(s32[1,1,16]{2,1,0:T(1,128)} %param.13) | copy-start | bytes 196
  115.5 131.5 %all-to-all-start.1 = ((bf16[2048,4,256]{0,2,1:T(8,128)(2,1)}), bf16[2048,4,256]{0,2,1:T(8,128)(2,1)}, u32[]{:S(2)}, u32[]{:S(2)}) async-start(bf16[2048,4,256]{0,2,1:T(8,128)(2,1)} %bitcast.122), calls=%async_computation.1 | async-start | bytes 8388608 | tf_op jit(solution)/shard_map/all_to_all | solution.py:143
  120.5 192.0 %all-gather.4.cloned.1.call-start = ((), (), s32[]{:S(2)}) async-start(), calls=%async_computation.2 | async-start | bytes 1179648 | tf_op jit(solution)/shard_map/all_gather | solution.py:16
  254.4 7.8 %copy-start.4 = (s32[128]{0:T(128)S(1)}, s32[128]{0:T(128)}, u32[]{:S(2)}) copy-start(s32[128]{0:T(128)} %param.16) | copy-start | bytes 1540
Sparse Core Ops, SparseCore 0:
  289.9 22.5 all-gather.3
where the time goes:
time: 332 us; the launch traced here: 331 us
  blocking collectives  128 us (39%)
  waiting for transfers between devices  86.7 us (26%)
  local copies, waits for them, and re-layouts  42.6 us (13%)
  matrix products  39 us (12%)
  between operations  14.2 us (4%)
  starting transfers between devices  10.4 us (3%)
  other arithmetic  10.1 us (3%)
    unnamed x1, blocking collectives  91 us
    all_to_all x1, waiting for transfers between devices, per_device(): lax.all_to_all(key_local.reshape(row_count, head_count, head_width), 'hea...  83.3 us
    all_gather x2, blocking collectives, combined_all(): everything = jax.tree.map(lambda part: lax.all_gather(part, axis), array)  18.9 us
    all_gather x1, blocking collectives, per_device(): all_queries = lax.all_gather(query_local, 'ctx', axis=0, tiled=True)  10.5 us
    dot_general x4, matrix products, per_block(): jnp.dot(weights.astype(jnp.bfloat16), value_head, preferred_element_type=...  10.4 us
    dot_general x4, matrix products, per_block(): jnp.einsum('qd,kd->qk', query_block, key_head, preferred_element_type=jnp...  10.1 us
    dot_general x1, matrix products, per_device(): jnp.dot(normed, w_value, preferred_element_type=jnp.float32)  9.62 us
    another operation x1, local copies, waits for them, and re-layouts, local_partials(): value_rows.reshape(key_count, heads_here, HD).transpose(1, 0, 2)  7.77 us
  transfers between devices with their start and end apart: 3, of which 2 were waited for; matrix products, arithmetic and copies ran while one was open for 8% of the time, Pallas kernels for 0%

commit v1 on v0

v1 whole, which is shorter than its diff:
```python
import functools

import jax
import jax.numpy as jnp
from jax import lax
from jax.experimental import pallas as pl
from jax.experimental.pallas import tpu as pltpu
from jax.sharding import PartitionSpec as P

HD = 64
BLOCK = 128
PAIR = 2 * HD
LANES = 128

PROJECT_ROWS = 512
AHEAD = 2
WEIGHT_PARTS = 1
ATTEND_ROWS = 256
ATTEND_GRANT = 57 * 2**20
VMEM_GRANT = 12 * 2**20

NEG_FILL = -1e30
EPSILON = 1e-06

FAR = 2**30

NT = (((1,), (1,)), ((), ()))


def normalize(source_rows):
    wide_rows = source_rows.astype(jnp.float32)
    factor = lax.rsqrt(jnp.mean(wide_rows * wide_rows, axis=-1, keepdims=True) + EPSILON)
    return (wide_rows * factor).astype(jnp.bfloat16)

VMEM = pl.BlockSpec(memory_space=pltpu.VMEM)
SMEM = pl.BlockSpec(memory_space=pltpu.SMEM)
HBM = pl.BlockSpec(memory_space=pltpu.HBM)


def query_kernel(latent_hbm, w_query_hbm, out_hbm, latent_ref, w_query_ref, query_ref, in_sem, out_sem):
    latent_copy = pltpu.make_async_copy(latent_hbm, latent_ref, in_sem.at[0])
    weight_copy = pltpu.make_async_copy(w_query_hbm, w_query_ref, in_sem.at[1])
    weight_copy.start()
    latent_copy.start()
    latent_copy.wait()
    normed = normalize(latent_ref[...])
    weight_copy.wait()
    query = jnp.dot(normed, w_query_ref[...], preferred_element_type=jnp.float32) * HD ** (-0.5)
    query_ref[...] = query.astype(jnp.bfloat16)
    copies = [
        pltpu.make_async_copy(query_ref, out_hbm.at[k], out_sem.at[k])
        for k in range(out_hbm.shape[0])
    ]
    for copy in copies:
        copy.start()
    for copy in copies:
        copy.wait()


def self_kernel(
    after_hbm, latent_ref, query_hbm, w_key_hbm, w_value_hbm, score_ref, value_ref, query_ref, key_ref, column_ref, sem
):
    latent_rows, width = query_ref.shape
    mine = pl.ds(pl.multiple_of(lax.axis_index("head") * width, width), width)
    query_copy = pltpu.make_async_copy(query_hbm.at[0], query_ref, sem.at[0])
    key_copy = pltpu.make_async_copy(w_key_hbm.at[:, mine], key_ref, sem.at[1])
    value_copy = pltpu.make_async_copy(w_value_hbm.at[:, mine], column_ref, sem.at[2])
    query_copy.start()
    key_copy.start()
    value_copy.start()
    normed = normalize(latent_ref[...])
    key_copy.wait()
    key = jnp.dot(normed, key_ref[...], preferred_element_type=jnp.float32).astype(jnp.bfloat16)
    query_copy.wait()
    products = query_ref[...].astype(jnp.float32) * key.astype(jnp.float32)
    for first in range(0, width, HD):
        score = jnp.sum(products[:, first : first + HD], axis=1, keepdims=True)
        score_ref[:, first : first + HD] = jnp.broadcast_to(score, (latent_rows, HD))
    value_copy.wait()
    value = jnp.dot(normed, column_ref[...], preferred_element_type=jnp.float32)
    value_ref[...] = value.astype(jnp.bfloat16)


def project_kernel(
    prefix_hbm, w_key_hbm, w_value_hbm, both_hbm, prefix_ref, w_key_ref, w_value_ref, both_ref, in_sem, out_sem, *, tile
):
    rows = prefix_ref.shape[0]
    pairs = both_ref.shape[1]
    row_copies = [
        pltpu.make_async_copy(
            prefix_hbm.at[pl.ds(r, tile)], prefix_ref.at[pl.ds(r, tile)], in_sem.at[r // tile]
        )
        for r in range(0, rows, tile)
    ]
    columns = w_key_ref.shape[1]
    width = columns // WEIGHT_PARTS

    def part_copies(hbm, ref, first):
        return [
            pltpu.make_async_copy(
                hbm.at[:, pl.ds(k * width, width)], ref.at[:, pl.ds(k * width, width)], in_sem.at[first + k]
            )
            for k in range(WEIGHT_PARTS)
        ]

    def project_rows(normed, ref, waits):
        parts = []
        for k in range(WEIGHT_PARTS):
            if waits:
                waits[k].wait()
            part = jnp.dot(
                normed, ref[:, k * width : (k + 1) * width], preferred_element_type=jnp.float32
            )
            parts.append(part.astype(jnp.bfloat16))
        return jnp.concatenate(parts, axis=1)

    first = rows // tile
    key_copies = part_copies(w_key_hbm, w_key_ref, first)
    value_copies = part_copies(w_value_hbm, w_value_ref, first + WEIGHT_PARTS)
    row_copies[0].start()
    for copy in key_copies + value_copies + row_copies[1:]:
        copy.start()
    out_copies = []
    for r in range(0, rows, tile):
        span = pl.ds(r, tile)
        k = r // tile
        row_copies[k].wait()
        normed = normalize(prefix_ref[r : r + tile, :])
        key = project_rows(normed, w_key_ref, key_copies if r == 0 else None)
        for p in range(pairs):
            both_ref[0, p, r : r + tile, :] = key[:, p * PAIR : (p + 1) * PAIR]
        copy = pltpu.make_async_copy(both_ref.at[0, :, span, :], both_hbm.at[0, :, span, :], out_sem.at[2 * k])
        copy.start()
        out_copies.append(copy)
        value = project_rows(normed, w_value_ref, value_copies if r == 0 else None)
        for p in range(pairs):
            for b in range(r, r + tile, BLOCK):
                both_ref[1, p, b : b + BLOCK, :] = value[b - r : b - r + BLOCK, p * PAIR : (p + 1) * PAIR].T
        copy = pltpu.make_async_copy(
            both_ref.at[1, :, span, :], both_hbm.at[1, :, span, :], out_sem.at[2 * k + 1]
        )
        copy.start()
        out_copies.append(copy)
    for copy in out_copies:
        copy.wait()


def attend_kernel(
    list_hbm, count_hbm, pos_hbm, query_ref, both_hbm, out_ref,
    list_ref, count_ref, pos_ref, start_ref, bias_ref, both_ref, even_ref, odd_ref, log_ref, small_sem, sem, *, chunk
):
    _, pairs, rows, _ = both_ref.shape
    tiles = bias_ref.shape[0]
    blocks = rows // BLOCK

    def fetch(pair):
        return (
            pltpu.make_async_copy(both_hbm.at[0, pair], both_ref.at[0, pair], sem.at[0, pair]),
            pltpu.make_async_copy(both_hbm.at[1, pair], both_ref.at[1, pair], sem.at[1, pair]),
        )

    small_copies = [
        pltpu.make_async_copy(list_hbm, list_ref, small_sem.at[0]),
        pltpu.make_async_copy(count_hbm, count_ref, small_sem.at[1]),
        pltpu.make_async_copy(pos_hbm, pos_ref, small_sem.at[2]),
    ]
    for copy in small_copies:
        copy.start()
    for p in range(min(AHEAD, pairs)):
        for copy in fetch(p):
            copy.start()
    for copy in small_copies:
        copy.wait()

    shard = lax.axis_index("ctx") * lax.axis_size("head") + lax.axis_index("head")
    for b in range(blocks):
        start_ref[b] = FAR
    for j in range(blocks):
        block = list_ref[0, 0, j]

        @pl.when(j < count_ref[0, 0])
        def _():
            start_ref[block] = (shard * blocks + block) * BLOCK

    row_iota = lax.broadcasted_iota(jnp.int32, (BLOCK, LANES), 0)
    for t in range(tiles):
        pos = pos_ref[:, t * LANES : (t + 1) * LANES]
        for b in range(blocks):
            allowed = row_iota < pos - start_ref[b]
            bias_ref[t, b * BLOCK : (b + 1) * BLOCK, :] = jnp.where(allowed, 0.0, NEG_FILL)

    ctx_count, head_count, latent_rows, head_width = query_ref.shape
    ctx_tile = LANES // latent_rows
    per_head = head_width // PAIR
    heads_here = head_width // HD
    steps = tiles * pairs
    half = lax.broadcasted_iota(jnp.int32, (LANES, PAIR), 1) < HD

    def place(step):
        tile, pair = step // pairs, step % pairs
        return tile, pair, pair // per_head, pair % per_head

    def spread_of(step):
        tile, _, group, j = place(step)
        query = query_ref[
            pl.ds(tile * ctx_tile, ctx_tile), group, :, pl.ds(pl.multiple_of(j * PAIR, PAIR), PAIR)
        ].reshape(LANES, PAIR)
        zero = jnp.zeros_like(query)
        return jnp.concatenate([jnp.where(half, query, zero), jnp.where(half, zero, query)], axis=0)

    def score_part(step, spread, r, store_ref, top8):
        tile, pair, _, _ = place(step)
        scores = lax.dot_general(
            both_ref[0, pair, r : r + chunk, :], spread, NT, preferred_element_type=jnp.float32
        )
        bias = bias_ref[tile, r : r + chunk, :]
        scores = scores + jnp.concatenate([bias, bias], axis=1)
        store_ref[r : r + chunk, :] = scores
        return jnp.maximum(top8, jnp.max(scores.reshape(chunk // 8, 8, 2 * LANES), axis=0))

    def weigh_part(step, r, load_ref, top, sum8, total):
        pair = place(step)[1]
        weights = jnp.exp(load_ref[r : r + chunk, :] - top)
        sum8 = sum8 + jnp.sum(weights.reshape(chunk // 8, 8, 2 * LANES), axis=0)
        values = [both_ref[1, pair, b : b + BLOCK, :] for b in range(r, r + chunk, BLOCK)]
        total = total + jnp.dot(
            jnp.concatenate(values, axis=1),
            weights.astype(jnp.bfloat16),
            preferred_element_type=jnp.float32,
        )
        return sum8, total

    def finish(step, top, sum8, total):
        tile, pair, group, j = place(step)
        sums = jnp.sum(sum8, axis=0, keepdims=True)
        scaled = total / sums
        own = jnp.concatenate([scaled[:HD, :LANES], scaled[HD:, LANES:]], axis=0)
        out_ref[
            pl.ds(tile * ctx_tile, ctx_tile),
            group,
            pl.ds(pl.multiple_of(j * latent_rows, latent_rows), latent_rows),
            :,
        ] = own.T.astype(jnp.bfloat16).reshape(ctx_tile, latent_rows, PAIR)
        log_sum = top + jnp.log(sums)
        log_ref[step] = jnp.concatenate([log_sum[:, :LANES], log_sum[:, LANES:]], axis=0)

    lowest = jnp.full((8, 2 * LANES), NEG_FILL, jnp.float32)
    none = jnp.zeros((8, 2 * LANES), jnp.float32)
    empty = jnp.zeros((PAIR, 2 * LANES), jnp.float32)
    chunks = range(0, rows, chunk)

    def arrive(step):
        @pl.when(step < pairs)
        def _():
            for copy in fetch(step):
                copy.wait()

        @pl.when(step + AHEAD < pairs)
        def _():
            for copy in fetch(step + AHEAD):
                copy.start()

    def both(step, store_ref, load_ref, top):
        arrive(step)
        spread = spread_of(step)
        top8, sum8, total = lowest, none, empty
        for r in chunks:
            top8 = score_part(step, spread, r, store_ref, top8)
            sum8, total = weigh_part(step - 1, r, load_ref, top, sum8, total)
        finish(step - 1, top, sum8, total)
        return jnp.max(top8, axis=0, keepdims=True)

    arrive(0)
    spread = spread_of(0)
    top8 = lowest
    for r in chunks:
        top8 = score_part(0, spread, r, even_ref, top8)
    top = jnp.max(top8, axis=0, keepdims=True)

    def turn(k, top):
        top = both(2 * k + 1, odd_ref, even_ref, top)
        return both(2 * k + 2, even_ref, odd_ref, top)

    top = lax.fori_loop(0, steps // 2 - 1, turn, top)
    top = both(steps - 1, odd_ref, even_ref, top)
    sum8, total = none, empty
    for r in chunks:
        sum8, total = weigh_part(steps - 1, r, odd_ref, top, sum8, total)
    finish(steps - 1, top, sum8, total)

    data_rows = per_head * latent_rows
    for tile in range(tiles):
        for group in range(head_count):
            logs = jnp.concatenate(
                [log_ref[tile * pairs + group * per_head + j] for j in range(per_head)], axis=0
            )
            high = logs.astype(jnp.bfloat16)
            low = logs - high.astype(jnp.float32)
            pieces = jnp.concatenate([high.astype(jnp.float32), low], axis=0).astype(jnp.bfloat16)
            for c in range(ctx_tile):
                out_ref[tile * ctx_tile + c, group, data_rows : data_rows + 2 * heads_here, :] = pieces


def project(prefix, w_key, w_value):
    rows, model = prefix.shape
    columns = w_key.shape[1]
    pairs = columns // PAIR
    small = prefix.dtype
    return pl.pallas_call(
        functools.partial(project_kernel, tile=PROJECT_ROWS),
        in_specs=[HBM] * 3,
        out_specs=HBM,
        out_shape=jax.ShapeDtypeStruct((2, pairs, rows, PAIR), small),
        scratch_shapes=[
            pltpu.VMEM(prefix.shape, small),
            pltpu.VMEM(w_key.shape, small),
            pltpu.VMEM(w_value.shape, small),
            pltpu.VMEM((2, pairs, rows, PAIR), small),
            pltpu.SemaphoreType.DMA((2 * WEIGHT_PARTS + rows // PROJECT_ROWS,)),
            pltpu.SemaphoreType.DMA((2 * (rows // PROJECT_ROWS),)),
        ],
        cost_estimate=pl.CostEstimate(
            flops=4 * rows * model * columns,
            bytes_accessed=2 * (rows * model + 2 * model * columns + 2 * rows * columns),
            transcendentals=0,
        ),
        name="project",
    )(prefix, w_key, w_value)


def attend(keep_blocks, keep_count, latent_pos, queries, both):
    ctx_count, head_count, latent_rows, head_width = queries.shape
    _, pairs, rows, _ = both.shape
    columns = pairs * PAIR
    latents = latent_pos.shape[0]
    tiles = latents // LANES
    heads_here = head_width // HD
    small = queries.dtype
    packed_rows = latent_rows * head_width // LANES + 2 * heads_here
    return pl.pallas_call(
        functools.partial(attend_kernel, chunk=ATTEND_ROWS),
        in_specs=[HBM, HBM, HBM, VMEM, HBM],
        out_specs=VMEM,
        out_shape=jax.ShapeDtypeStruct((ctx_count, head_count, packed_rows, LANES), small),
        scratch_shapes=[
            pltpu.SMEM(keep_blocks.shape, jnp.int32),
            pltpu.SMEM(keep_count.shape, jnp.int32),
            pltpu.VMEM((1, latents), jnp.int32),
            pltpu.SMEM((rows // BLOCK,), jnp.int32),
            pltpu.VMEM((tiles, rows, LANES), jnp.float32),
            pltpu.VMEM((2, pairs, rows, PAIR), small),
            pltpu.VMEM((rows, 2 * LANES), jnp.float32),
            pltpu.VMEM((rows, 2 * LANES), jnp.float32),
            pltpu.VMEM((tiles * pairs, 2, LANES), jnp.float32),
            pltpu.SemaphoreType.DMA((3,)),
            pltpu.SemaphoreType.DMA((2, pairs)),
        ],
        compiler_params=pltpu.CompilerParams(vmem_limit_bytes=ATTEND_GRANT),
        cost_estimate=pl.CostEstimate(
            flops=16 * rows * columns * latents,
            bytes_accessed=4 * rows * columns,
            transcendentals=rows * columns * latents // HD,
        ),
        name="attend",
    )(keep_blocks, keep_count, latent_pos.reshape(1, latents), queries, both)


def join_kernel(parts_ref, self_score_ref, self_value_ref, out_ref, turned_ref):
    sources = parts_ref.shape[0]
    latent_rows, width = out_ref.shape
    heads = width // HD
    per_head = width // PAIR
    data_rows = per_head * latent_rows
    wide = parts_ref[:, data_rows:, :].astype(jnp.float32)
    logs = wide + pltpu.roll(wide, heads, 1)
    top = jnp.max(logs, axis=0)
    weights = jnp.exp(logs - top[None])
    sums = jnp.sum(weights, axis=0)
    turned_ref[:, : sources * 8] = weights.reshape(sources * 8, LANES).T
    filler = jnp.zeros((LANES - 16, LANES), jnp.float32)
    turned_ref[:, sources * 8 :] = jnp.concatenate([top, sums, filler], axis=0).T
    lane = (lax.axis_index("ctx") * latent_rows) % LANES
    mine = turned_ref[pl.ds(pl.multiple_of(lane, 8), latent_rows), :]
    half = lax.broadcasted_iota(jnp.int32, (latent_rows, PAIR), 1) < HD

    def widen(first):
        left = jnp.broadcast_to(mine[:, first : first + 1], (latent_rows, PAIR))
        right = jnp.broadcast_to(mine[:, first + 1 : first + 2], (latent_rows, PAIR))
        return jnp.where(half, left, right)

    for j in range(per_head):
        columns = slice(j * PAIR, (j + 1) * PAIR)
        total = jnp.zeros((latent_rows, PAIR), jnp.float32)
        for s in range(sources):
            part = parts_ref[s, j * latent_rows : (j + 1) * latent_rows, :].astype(jnp.float32)
            total = total + widen(8 * s + 2 * j) * part
        kept_top = widen(8 * sources + 2 * j)
        kept_sum = widen(8 * sources + 8 + 2 * j)
        self_score = self_score_ref[:, columns]
        final_top = jnp.maximum(kept_top, self_score)
        keep = jnp.exp(kept_top - final_top)
        self_weight = jnp.exp(self_score - final_top)
        denominator = kept_sum * keep + self_weight
        numerator = total * keep + self_weight * self_value_ref[:, columns].astype(jnp.float32)
        out_ref[:, columns] = (numerator / denominator).astype(jnp.bfloat16)


def per_device(prefix, keep_blocks, keep_count, latent_inputs, latent_pos, w_query, w_key, w_value):
    head_count = lax.axis_size("head")
    ctx_count = lax.axis_size("ctx")
    device_count = head_count * ctx_count
    head_width = w_query.shape[1]
    model = prefix.shape[1]
    latent_rows = latent_inputs.shape[0]
    axes = ("ctx", "head")
    small = jnp.bfloat16

    copies = pl.pallas_call(
        query_kernel,
        in_specs=[HBM] * 2,
        out_specs=HBM,
        out_shape=jax.ShapeDtypeStruct((device_count, latent_rows, head_width), small),
        scratch_shapes=[
            pltpu.VMEM(latent_inputs.shape, small),
            pltpu.VMEM(w_query.shape, small),
            pltpu.VMEM((latent_rows, head_width), small),
            pltpu.SemaphoreType.DMA((2,)),
            pltpu.SemaphoreType.DMA((device_count,)),
        ],
        name="query",
    )(latent_inputs, w_query)
    queries = lax.all_to_all(copies, axes, split_axis=0, concat_axis=0, tiled=True)
    queries = queries.reshape(ctx_count, head_count, latent_rows, head_width)

    both = project(prefix, w_key, w_value)
    packed = attend(keep_blocks, keep_count, latent_pos, queries, both)
    packed_rows = packed.shape[2]
    arrived = lax.all_to_all(
        packed.reshape(device_count, packed_rows, LANES), axes, split_axis=0, concat_axis=0, tiled=True
    )

    self_score, self_value = pl.pallas_call(
        self_kernel,
        in_specs=[HBM, VMEM, HBM, HBM, HBM],
        out_specs=[VMEM] * 2,
        out_shape=[
            jax.ShapeDtypeStruct((latent_rows, head_width), jnp.float32),
            jax.ShapeDtypeStruct((latent_rows, head_width), small),
        ],
        scratch_shapes=[
            pltpu.VMEM((latent_rows, head_width), small),
            pltpu.VMEM((model, head_width), small),
            pltpu.VMEM((model, head_width), small),
            pltpu.SemaphoreType.DMA((3,)),
        ],
        compiler_params=pltpu.CompilerParams(vmem_limit_bytes=VMEM_GRANT),
        cost_estimate=pl.CostEstimate(
            flops=4 * latent_rows * model * head_width,
            bytes_accessed=4 * model * head_width,
            transcendentals=0,
        ),
        name="own",
    )(packed, latent_inputs, copies, w_key, w_value)

    return pl.pallas_call(
        join_kernel,
        in_specs=[VMEM] * 3,
        out_specs=VMEM,
        out_shape=jax.ShapeDtypeStruct((latent_rows, head_width), small),
        scratch_shapes=[pltpu.VMEM((LANES, device_count * 8 + LANES), jnp.float32)],
        compiler_params=pltpu.CompilerParams(vmem_limit_bytes=VMEM_GRANT),
        name="join",
    )(arrived, self_score, self_value)


def solution(mesh):
    return jax.shard_map(
        per_device,
        mesh=mesh,
        in_specs=(
            P(("ctx", "head"), None),
            P("head", "ctx", None),
            P("head", "ctx"),
            P("ctx", None),
            P(),
            P(None, "head"),
            P(),
            P(),
        ),
        out_specs=P("ctx", "head"),
        check_vma=False,
    )
```

time: 332 us -> 52.7 us (0.16)
  blocking collectives: 128 us -> 0 us
  waiting for transfers between devices: 86.7 us -> 8.09 us
  local copies, waits for them, and re-layouts: 42.6 us -> 3.3 us
  matrix products: 39 us -> 0 us
  Pallas kernels: 0 us -> 27.2 us
  between operations: 14.2 us -> 0.75 us
  other arithmetic: 10.1 us -> 0 us
    unnamed x1 -> x0, blocking collectives: 91 us -> none
    all_to_all x2, waiting for transfers between devices: 83.3 us -> 8.09 us  [the longest x1 8.09 us: per_device(): lax.all_to_all(packed.reshape(device_count, packed_rows, LANES), axes, sp...]
    dot_general x13 -> x0, matrix products: 39 us -> none  [the longest x4 10.4 us: per_block(): jnp.dot(weights.astype(jnp.bfloat16), value_head, preferred_element_type=...]
    all_gather x4 -> x0, blocking collectives: 36.6 us -> none  [the longest x2 18.9 us: combined_all(): everything = jax.tree.map(lambda part: lax.all_gather(part, axis), array)]
    pallas_call x0 -> x5, Pallas kernels: none -> 27.2 us  [the longest x1 13.5 us: project(): pl.pallas_call(functools.partial(project_kernel, tile=PROJECT_ROWS), in_s...]
    another operation x3 -> x0, local copies, waits for them, and re-layouts: 16.3 us -> none  [the longest x1 7.77 us: local_partials(): value_rows.reshape(key_count, heads_here, HD).transpose(1, 0, 2)]
    all_to_all x2 -> x0, local copies, waits for them, and re-layouts: 14.8 us -> none  [the longest x1 7.4 us: per_device(): lax.all_to_all(value_local.reshape(row_count, head_count, head_width), 'h...]
    reduce_sum x7 -> x0, other arithmetic: 9.04 us -> none  [the longest x4 5.6 us: per_block(): weight_sum = jnp.sum(weights, axis=1)]
  transfers between devices with their start and end apart: 3 -> 2, of which waited for: 2 -> 1; matrix products, arithmetic and copies ran while one was open for 8% -> 0% of each run, Pallas kernels for 0% -> 28%
where the time goes in v1:
time: 52.7 us; the launch traced here: 52.3 us
  Pallas kernels  27.2 us (52%)
  starting transfers between devices  12.9 us (24%)
  waiting for transfers between devices  8.09 us (15%)
  local copies, waits for them, and re-layouts  3.3 us (6%)
  between operations  0.75 us (1%)
    pallas_call x1, Pallas kernels, project(): pl.pallas_call(functools.partial(project_kernel, tile=PROJECT_ROWS), in_s...  13.5 us
    pallas_call x1, Pallas kernels, attend(): pl.pallas_call(functools.partial(attend_kernel, chunk=ATTEND_ROWS), in_sp...  9.23 us
    all_to_all x1, waiting for transfers between devices, per_device(): lax.all_to_all(packed.reshape(device_count, packed_rows, LANES), axes, sp...  8.09 us
    all_to_all x1, starting transfers between devices, per_device(): lax.all_to_all(copies, axes, split_axis=0, concat_axis=0, tiled=True)  7.09 us
    all_to_all x1, starting transfers between devices, per_device(): lax.all_to_all(packed.reshape(device_count, packed_rows, LANES), axes, sp...  5.83 us
    unnamed x12, local copies, waits for them, and re-layouts  3.3 us
    pallas_call x1, Pallas kernels, per_device(): pl.pallas_call(query_kernel, in_specs=[HBM] * 2, out_specs=HBM, out_shape...  2.26 us
    pallas_call x1, Pallas kernels, per_device(): pl.pallas_call(join_kernel, in_specs=[VMEM] * 3, out_specs=VMEM, out_shap...  1.32 us
  transfers between devices with their start and end apart: 2, of which 1 were waited for; matrix products, arithmetic and copies ran while one was open for 0% of the time, Pallas kernels for 28%

profile of v1, /device:TPU:1, one launch (start us, length us, event | category | flops | bytes accessed | tf_op | source)
XLA Modules:
  0.0 52.3 jit_solution(41293562148576237)
XLA Ops:
  0.0 2.3 %query.1.query_hbm = bf16[32,16,256]{2,1,0:T(8,128)(2,1)} custom-call(bf16[16,1024]{1,0:T(8,128)(2,1)} %latent_ref.1, bf16[1024,256]{1,0:T(8,128)(2,1)} %w_query_hbm.1), custom_call_target="tpu_custom_call" | custom-call | tf_op jit(solution)/shard_map/query/pallas_call | solution.py:418
  2.3 7.1 %all-to-all-start = ((bf16[32,16,256]{2,1,0:T(8,128)(2,1)}), bf16[32,16,256]{2,1,0:T(8,128)(2,1)S(1)}, u32[]{:S(2)}, u32[]{:S(2)}) async-start(bf16[32,16,256]{2,1,0:T(8,128)(2,1)} %query.1.query_hbm), calls=%async_computation | async-start | bytes 524288 | tf_op jit(solution)/shard_map/all_to_all | solution.py:432
  10.0 13.5 %project.1.both_hbm = bf16[2,8,2048,128]{3,2,1,0:T(8,128)(2,1)} custom-call(bf16[2048,1024]{1,0:T(8,128)(2,1)} %prefix_hbm.1, bf16[1024,1024]{1,0:T(8,128)(2,1)} %w_key_hbm.3, bf16[1024,1024]{1,0:T(8,128)(2,1)} %w_value_hbm.3), custom_call_target="tpu_custom_call" | custom-call | flops 8589934592 | bytes 16777216 | tf_op jit(solution)/shard_map/project/pallas_call | solution.py:309
  23.5 0.0 all-to-all-done
  23.5 0.0 copy-start.5
  23.5 0.7 %copy-done.5 = bf16[32,16,256]{2,1,0:T(8,128)(2,1)} copy-done((bf16[32,16,256]{2,1,0:T(8,128)(2,1)}, bf16[32,16,256]{2,1,0:T(8,128)(2,1)S(1)}, u32[]{:S(2)}) %copy-start.5) | copy-done | bytes 262168
  24.3 0.0 copy-start
  24.3 0.0 copy-start.1
  24.3 0.0 copy-start.4
  24.3 9.2 %attend.1.after_hbm = bf16[8,4,40,128]{3,2,1,0:T(8,128)(2,1)} custom-call(s32[1,1,16]{2,1,0:T(1,128)} %list_hbm.1, s32[1,1]{1,0:T(1,128)S(6)} %copy.9.count_hbm, s32[1,128]{1,0:T(1,128)} %bitcast.5, bf16[8,4,16,256]{3,2,1,0:T(8,128)(2,1)} %bitcast.4, bf16[2,8,2048,128]{3,2,1,0:T(8,128)(2,1)} %project.1.both_hbm), custom_call_target="tpu_custom_call" | custom-call | flops 4294967296 | bytes 8388608 | tf_op jit(solution)/shard_map/attend/pallas_call | solution.py:340
  33.5 5.8 %all-to-all-start.1 = ((bf16[32,40,128]{2,1,0:T(8,128)(2,1)}), bf16[32,40,128]{2,1,0:T(8,128)(2,1)S(1)}, u32[]{:S(2)}, u32[]{:S(2)}) async-start(bf16[32,40,128]{2,1,0:T(8,128)(2,1)} %bitcast.3), calls=%async_computation.1 | async-start | bytes 655360 | tf_op jit(solution)/shard_map/all_to_all | solution.py:438
  39.3 0.0 copy-done
  39.4 0.0 copy-done.1
  39.4 0.0 copy-done.4
  39.4 0.0 copy-start.2
  39.4 1.6 %copy-done.2 = bf16[1024,1024]{1,0:T(8,128)(2,1)S(1)} copy-done((bf16[1024,1024]{1,0:T(8,128)(2,1)S(1)}, bf16[1024,1024]{1,0:T(8,128)(2,1)}, u32[]{:S(2)}) %copy-start.2) | copy-done | bytes 2097176
  41.0 0.0 copy-start.3
  41.0 1.0 %copy-done.3 = bf16[8,4,40,128]{3,2,1,0:T(8,128)(2,1)S(1)} copy-done((bf16[8,4,40,128]{3,2,1,0:T(8,128)(2,1)S(1)}, bf16[8,4,40,128]{3,2,1,0:T(8,128)(2,1)}, u32[]{:S(2)}) %copy-start.3) | copy-done | bytes 327704
  41.9 0.9 %own.1 = (f32[16,256]{1,0:T(8,128)S(1)}, bf16[16,256]{1,0:T(8,128)(2,1)S(1)}) custom-call(bf16[8,4,40,128]{3,2,1,0:T(8,128)(2,1)S(1)} %copy-done.3, bf16[16,1024]{1,0:T(8,128)(2,1)S(1)} %copy-done.4, bf16[32,16,256]{2,1,0:T(8,128)(2,1)S(1)} %copy-done, bf16[1024,1024]{1,0:T(8,128)(2,1)S(1)} %copy-done.1, bf16[1024,1024]{1,0:T(8,128)(2,1)S(1)} %copy-done.2), custom_call_target="tpu_custom_call" | custom-call | flops 16777216 | bytes 1048576 | tf_op jit(solution)/shard_map/own/pallas_call | solution.py:442
  42.9 8.1 %all-to-all-done.1.parts_ref = bf16[32,40,128]{2,1,0:T(8,128)(2,1)S(1)} async-done(((bf16[32,40,128]{2,1,0:T(8,128)(2,1)}), bf16[32,40,128]{2,1,0:T(8,128)(2,1)S(1)}, u32[]{:S(2)}, u32[]{:S(2)}) %all-to-all-start.1) | async-done | bytes 327712 | tf_op jit(solution)/shard_map/all_to_all | solution.py:438
  51.0 1.3 %join.1 = bf16[16,256]{1,0:T(8,128)(2,1)} custom-call(bf16[32,40,128]{2,1,0:T(8,128)(2,1)S(1)} %all-to-all-done.1.parts_ref, f32[16,256]{1,0:T(8,128)S(1)} %get-tuple-element.7.self_score_ref, bf16[16,256]{1,0:T(8,128)(2,1)S(1)} %get-tuple-element.8.self_value_ref), custom_call_target="tpu_custom_call" | custom-call | tf_op jit(solution)/shard_map/join/pallas_call | solution.py:465
Async XLA Ops:
  2.3 21.2 %all-to-all-start = ((bf16[32,16,256]{2,1,0:T(8,128)(2,1)}), bf16[32,16,256]{2,1,0:T(8,128)(2,1)S(1)}, u32[]{:S(2)}, u32[]{:S(2)}) async-start(bf16[32,16,256]{2,1,0:T(8,128)(2,1)} %query.1.query_hbm), calls=%async_computation | async-start | bytes 524288 | tf_op jit(solution)/shard_map/all_to_all | solution.py:432
  23.5 0.7 %copy-start.5 = (bf16[32,16,256]{2,1,0:T(8,128)(2,1)}, bf16[32,16,256]{2,1,0:T(8,128)(2,1)S(1)}, u32[]{:S(2)}) copy-start(bf16[32,16,256]{2,1,0:T(8,128)(2,1)S(1)} %all-to-all-done) | copy-start | bytes 786436
  24.3 15.1 %copy-start = (bf16[32,16,256]{2,1,0:T(8,128)(2,1)S(1)}, bf16[32,16,256]{2,1,0:T(8,128)(2,1)}, u32[]{:S(2)}) copy-start(bf16[32,16,256]{2,1,0:T(8,128)(2,1)} %query.1.query_hbm) | copy-start | bytes 786436
  24.3 15.1 %copy-start.1 = (bf16[1024,1024]{1,0:T(8,128)(2,1)S(1)}, bf16[1024,1024]{1,0:T(8,128)(2,1)}, u32[]{:S(2)}) copy-start(bf16[1024,1024]{1,0:T(8,128)(2,1)} %w_key_hbm.3) | copy-start | bytes 6291460
  24.3 15.1 %copy-start.4 = (bf16[16,1024]{1,0:T(8,128)(2,1)S(1)}, bf16[16,1024]{1,0:T(8,128)(2,1)}, u32[]{:S(2)}) copy-start(bf16[16,1024]{1,0:T(8,128)(2,1)} %latent_ref.1) | copy-start | bytes 98308
  33.5 17.5 %all-to-all-start.1 = ((bf16[32,40,128]{2,1,0:T(8,128)(2,1)}), bf16[32,40,128]{2,1,0:T(8,128)(2,1)S(1)}, u32[]{:S(2)}, u32[]{:S(2)}) async-start(bf16[32,40,128]{2,1,0:T(8,128)(2,1)} %bitcast.3), calls=%async_computation.1 | async-start | bytes 655360 | tf_op jit(solution)/shard_map/all_to_all | solution.py:438
  39.4 1.6 %copy-start.2 = (bf16[1024,1024]{1,0:T(8,128)(2,1)S(1)}, bf16[1024,1024]{1,0:T(8,128)(2,1)}, u32[]{:S(2)}) copy-start(bf16[1024,1024]{1,0:T(8,128)(2,1)} %w_value_hbm.3) | copy-start | bytes 6291460
  41.0 1.0 %copy-start.3 = (bf16[8,4,40,128]{3,2,1,0:T(8,128)(2,1)S(1)}, bf16[8,4,40,128]{3,2,1,0:T(8,128)(2,1)}, u32[]{:S(2)}) copy-start(bf16[8,4,40,128]{3,2,1,0:T(8,128)(2,1)} %attend.1.after_hbm) | copy-start | bytes 983044

commit v2 on v1

--- a/solution.py
+++ b/solution.py
@@ -16,7 +16,7 @@
 AHEAD = 2
 WEIGHT_PARTS = 1
 ATTEND_ROWS = 256
-ATTEND_GRANT = 57 * 2**20
+ATTEND_GRANT = 50 * 2**20
 VMEM_GRANT = 12 * 2**20
 
 NEG_FILL = -1e30
@@ -146,8 +146,8 @@
 
 
 def attend_kernel(
-    list_hbm, count_hbm, pos_hbm, query_ref, both_hbm, out_ref,
-    list_ref, count_ref, pos_ref, start_ref, bias_ref, both_ref, even_ref, odd_ref, log_ref, small_sem, sem, *, chunk
+    count_ref, pos_ref, query_ref, list_hbm, both_hbm, out_hbm,
+    list_ref, bias_ref, both_ref, even_ref, odd_ref, log_ref, out_ref, list_sem, sem, out_sem, *, chunk
 ):
     _, pairs, rows, _ = both_ref.shape
     tiles = bias_ref.shape[0]
@@ -159,42 +159,37 @@
             pltpu.make_async_copy(both_hbm.at[1, pair], both_ref.at[1, pair], sem.at[1, pair]),
         )
 
-    small_copies = [
-        pltpu.make_async_copy(list_hbm, list_ref, small_sem.at[0]),
-        pltpu.make_async_copy(count_hbm, count_ref, small_sem.at[1]),
-        pltpu.make_async_copy(pos_hbm, pos_ref, small_sem.at[2]),
-    ]
-    for copy in small_copies:
-        copy.start()
+    list_copy = pltpu.make_async_copy(list_hbm, list_ref, list_sem)
+    list_copy.start()
     for p in range(min(AHEAD, pairs)):
         for copy in fetch(p):
             copy.start()
-    for copy in small_copies:
-        copy.wait()
-
     shard = lax.axis_index("ctx") * lax.axis_size("head") + lax.axis_index("head")
-    for b in range(blocks):
-        start_ref[b] = FAR
+    count = jnp.broadcast_to(count_ref[...], (BLOCK, LANES))
+    row_iota = lax.broadcasted_iota(jnp.int32, (BLOCK, LANES), 0)
+    list_copy.wait()
     for j in range(blocks):
         block = list_ref[0, 0, j]
-
-        @pl.when(j < count_ref[0, 0])
-        def _():
-            start_ref[block] = (shard * blocks + block) * BLOCK
-
-    row_iota = lax.broadcasted_iota(jnp.int32, (BLOCK, LANES), 0)
-    for t in range(tiles):
-        pos = pos_ref[:, t * LANES : (t + 1) * LANES]
-        for b in range(blocks):
-            allowed = row_iota < pos - start_ref[b]
-            bias_ref[t, b * BLOCK : (b + 1) * BLOCK, :] = jnp.where(allowed, 0.0, NEG_FILL)
-
+        span = pl.ds(pl.multiple_of(block * BLOCK, BLOCK), BLOCK)
+        start = (shard * blocks + block) * BLOCK
+        for t in range(tiles):
+            pos = pos_ref[:, t * LANES : (t + 1) * LANES]
+            allowed = jnp.logical_and(row_iota < pos - start, count > j)
+            bias_ref[t, span, :] = jnp.where(allowed, 0.0, NEG_FILL)
     ctx_count, head_count, latent_rows, head_width = query_ref.shape
     ctx_tile = LANES // latent_rows
     per_head = head_width // PAIR
     heads_here = head_width // HD
     steps = tiles * pairs
     half = lax.broadcasted_iota(jnp.int32, (LANES, PAIR), 1) < HD
+
+    data_rows = per_head * latent_rows
+
+    def send(tile, group):
+        span = pl.ds(tile * ctx_tile, ctx_tile)
+        return pltpu.make_async_copy(
+            out_ref.at[span, group], out_hbm.at[span, group], out_sem.at[tile, group]
+        )
 
     def place(step):
         tile, pair = step // pairs, step % pairs
@@ -242,7 +237,20 @@
             :,
         ] = own.T.astype(jnp.bfloat16).reshape(ctx_tile, latent_rows, PAIR)
         log_sum = top + jnp.log(sums)
-        log_ref[step] = jnp.concatenate([log_sum[:, :LANES], log_sum[:, LANES:]], axis=0)
+        log_ref[j] = jnp.concatenate([log_sum[:, :LANES], log_sum[:, LANES:]], axis=0)
+
+    def depart(step):
+        tile, _, group, j = place(step)
+
+        @pl.when(j == per_head - 1)
+        def _():
+            logs = jnp.concatenate([log_ref[k] for k in range(per_head)], axis=0)
+            high = logs.astype(jnp.bfloat16)
+            low = logs - high.astype(jnp.float32)
+            pieces = jnp.concatenate([high.astype(jnp.float32), low], axis=0).astype(jnp.bfloat16)
+            for c in range(ctx_tile):
+                out_ref[tile * ctx_tile + c, group, data_rows : data_rows + 2 * heads_here, :] = pieces
+            send(tile, group).start()
 
     lowest = jnp.full((8, 2 * LANES), NEG_FILL, jnp.float32)
     none = jnp.zeros((8, 2 * LANES), jnp.float32)
@@ -268,6 +276,7 @@
             top8 = score_part(step, spread, r, store_ref, top8)
             sum8, total = weigh_part(step - 1, r, load_ref, top, sum8, total)
         finish(step - 1, top, sum8, total)
+        depart(step - 1)
         return jnp.max(top8, axis=0, keepdims=True)
 
     arrive(0)
@@ -287,18 +296,11 @@
     for r in chunks:
         sum8, total = weigh_part(steps - 1, r, odd_ref, top, sum8, total)
     finish(steps - 1, top, sum8, total)
-
-    data_rows = per_head * latent_rows
+    depart(steps - 1)
+
     for tile in range(tiles):
         for group in range(head_count):
-            logs = jnp.concatenate(
-                [log_ref[tile * pairs + group * per_head + j] for j in range(per_head)], axis=0
-            )
-            high = logs.astype(jnp.bfloat16)
-            low = logs - high.astype(jnp.float32)
-            pieces = jnp.concatenate([high.astype(jnp.float32), low], axis=0).astype(jnp.bfloat16)
-            for c in range(ctx_tile):
-                out_ref[tile * ctx_tile + c, group, data_rows : data_rows + 2 * heads_here, :] = pieces
+            send(tile, group).wait()
 
 
 def project(prefix, w_key, w_value):
@@ -339,21 +341,20 @@
     packed_rows = latent_rows * head_width // LANES + 2 * heads_here
     return pl.pallas_call(
         functools.partial(attend_kernel, chunk=ATTEND_ROWS),
-        in_specs=[HBM, HBM, HBM, VMEM, HBM],
-        out_specs=VMEM,
+        in_specs=[VMEM, VMEM, VMEM, HBM, HBM],
+        out_specs=HBM,
         out_shape=jax.ShapeDtypeStruct((ctx_count, head_count, packed_rows, LANES), small),
         scratch_shapes=[
             pltpu.SMEM(keep_blocks.shape, jnp.int32),
-            pltpu.SMEM(keep_count.shape, jnp.int32),
-            pltpu.VMEM((1, latents), jnp.int32),
-            pltpu.SMEM((rows // BLOCK,), jnp.int32),
             pltpu.VMEM((tiles, rows, LANES), jnp.float32),
             pltpu.VMEM((2, pairs, rows, PAIR), small),
             pltpu.VMEM((rows, 2 * LANES), jnp.float32),
             pltpu.VMEM((rows, 2 * LANES), jnp.float32),
-            pltpu.VMEM((tiles * pairs, 2, LANES), jnp.float32),
-            pltpu.SemaphoreType.DMA((3,)),
+            pltpu.VMEM((head_width // PAIR, 2, LANES), jnp.float32),
+            pltpu.VMEM((ctx_count, head_count, packed_rows, LANES), small),
+            pltpu.SemaphoreType.DMA,
             pltpu.SemaphoreType.DMA((2, pairs)),
+            pltpu.SemaphoreType.DMA((tiles, head_count)),
         ],
         compiler_params=pltpu.CompilerParams(vmem_limit_bytes=ATTEND_GRANT),
         cost_estimate=pl.CostEstimate(
@@ -362,7 +363,7 @@
             transcendentals=rows * columns * latents // HD,
         ),
         name="attend",
-    )(keep_blocks, keep_count, latent_pos.reshape(1, latents), queries, both)
+    )(keep_count, latent_pos.reshape(1, latents), queries, keep_blocks, both)
 
 
 def join_kernel(parts_ref, self_score_ref, self_value_ref, out_ref, turned_ref):

time: 52.7 us -> 50.9 us (0.966)
  local copies, waits for them, and re-layouts: 3.3 us -> 1.62 us
  Pallas kernels: 27.2 us -> 26.2 us
  waiting for transfers between devices: 8.09 us -> 9.06 us
    unnamed x12, local copies, waits for them, and re-layouts: 3.3 us -> 1.62 us
    pallas_call x1, Pallas kernels: 9.23 us -> 8.18 us  [attend(): pl.pallas_call(functools.partial(attend_kernel, chunk=ATTEND_ROWS), in_sp...]
    all_to_all x1, waiting for transfers between devices: 8.09 us -> 9.06 us  [per_device(): lax.all_to_all(packed.reshape(device_count, packed_rows, LANES), axes, sp...]
where the time goes in v2:
time: 50.9 us; the launch traced here: 50.6 us
  Pallas kernels  26.2 us (51%)
  starting transfers between devices  12.9 us (25%)
  waiting for transfers between devices  9.06 us (18%)
  local copies, waits for them, and re-layouts  1.62 us (3%)
  between operations  0.79 us (2%)
    pallas_call x1, Pallas kernels, project(): pl.pallas_call(functools.partial(project_kernel, tile=PROJECT_ROWS), in_s...  13.5 us
    all_to_all x1, waiting for transfers between devices, per_device(): lax.all_to_all(packed.reshape(device_count, packed_rows, LANES), axes, sp...  9.06 us
    pallas_call x1, Pallas kernels, attend(): pl.pallas_call(functools.partial(attend_kernel, chunk=ATTEND_ROWS), in_sp...  8.18 us
    all_to_all x1, starting transfers between devices, per_device(): lax.all_to_all(copies, axes, split_axis=0, concat_axis=0, tiled=True)  7.09 us
    all_to_all x1, starting transfers between devices, per_device(): lax.all_to_all(packed.reshape(device_count, packed_rows, LANES), axes, sp...  5.83 us
    pallas_call x1, Pallas kernels, per_device(): pl.pallas_call(query_kernel, in_specs=[HBM] * 2, out_specs=HBM, out_shape...  2.26 us
    unnamed x12, local copies, waits for them, and re-layouts  1.62 us
    pallas_call x1, Pallas kernels, per_device(): pl.pallas_call(join_kernel, in_specs=[VMEM] * 3, out_specs=VMEM, out_shap...  1.32 us
  transfers between devices with their start and end apart: 2, of which 1 were waited for; matrix products, arithmetic and copies ran while one was open for 0% of the time, Pallas kernels for 28%

profile of v2, /device:TPU:1, one launch (start us, length us, event | category | flops | bytes accessed | tf_op | source)
XLA Modules:
  0.0 50.6 jit_solution(5246149790947878459)
XLA Ops:
  0.0 2.3 %query.1.query_hbm = bf16[32,16,256]{2,1,0:T(8,128)(2,1)} custom-call(bf16[16,1024]{1,0:T(8,128)(2,1)} %latent_ref.1, bf16[1024,256]{1,0:T(8,128)(2,1)} %w_query_hbm.1), custom_call_target="tpu_custom_call" | custom-call | tf_op jit(solution)/shard_map/query/pallas_call | solution.py:419
  2.3 7.1 %all-to-all-start = ((bf16[32,16,256]{2,1,0:T(8,128)(2,1)}), bf16[32,16,256]{2,1,0:T(8,128)(2,1)S(1)}, u32[]{:S(2)}, u32[]{:S(2)}) async-start(bf16[32,16,256]{2,1,0:T(8,128)(2,1)} %query.1.query_hbm), calls=%async_computation | async-start | bytes 524288 | tf_op jit(solution)/shard_map/all_to_all | solution.py:433
  10.0 0.0 copy-start.4
  10.0 0.0 copy-start.5
  10.0 13.5 %project.1.both_hbm = bf16[2,8,2048,128]{3,2,1,0:T(8,128)(2,1)} custom-call(bf16[2048,1024]{1,0:T(8,128)(2,1)} %prefix_hbm.1, bf16[1024,1024]{1,0:T(8,128)(2,1)} %w_key_hbm.3, bf16[1024,1024]{1,0:T(8,128)(2,1)} %w_value_hbm.3), custom_call_target="tpu_custom_call" | custom-call | flops 8589934592 | bytes 16777216 | tf_op jit(solution)/shard_map/project/pallas_call | solution.py:311
  23.5 0.0 all-to-all-done
  23.5 0.0 copy-done.4
  23.6 0.0 copy-done.5
  23.6 0.0 copy-start
  23.6 0.0 copy-start.1
  23.6 0.0 copy-start.3
  23.6 8.2 %attend.1.after_hbm = bf16[8,4,40,128]{3,2,1,0:T(8,128)(2,1)} custom-call(s32[1,1]{1,0:T(1,128)S(6)} %copy.9.count_ref, s32[1,128]{1,0:T(1,128)S(1)} %bitcast.4, bf16[8,4,16,256]{3,2,1,0:T(8,128)(2,1)S(1)} %bitcast.3, s32[1,1,16]{2,1,0:T(1,128)S(1)} %copy-done.5, bf16[2,8,2048,128]{3,2,1,0:T(8,128)(2,1)} %project.1.both_hbm), custom_call_target="tpu_custom_call" | custom-call | flops 4294967296 | bytes 8388608 | tf_op jit(solution)/shard_map/attend/pallas_call | solution.py:342
  31.8 5.8 %all-to-all-start.1 = ((bf16[32,40,128]{2,1,0:T(8,128)(2,1)}), bf16[32,40,128]{2,1,0:T(8,128)(2,1)S(1)}, u32[]{:S(2)}, u32[]{:S(2)}) async-start(bf16[32,40,128]{2,1,0:T(8,128)(2,1)} %bitcast.2), calls=%async_computation.1 | async-start | bytes 655360 | tf_op jit(solution)/shard_map/all_to_all | solution.py:439
  37.6 0.0 copy-done
  37.6 0.0 copy-done.1
  37.6 0.0 copy-done.3
  37.7 0.0 copy-start.2
  37.7 1.6 %copy-done.2 = bf16[1024,1024]{1,0:T(8,128)(2,1)S(1)} copy-done((bf16[1024,1024]{1,0:T(8,128)(2,1)S(1)}, bf16[1024,1024]{1,0:T(8,128)(2,1)}, u32[]{:S(2)}) %copy-start.2) | copy-done | bytes 2097176
  39.2 0.9 %own.1 = (f32[16,256]{1,0:T(8,128)S(1)}, bf16[16,256]{1,0:T(8,128)(2,1)S(1)}) custom-call(bf16[8,4,40,128]{3,2,1,0:T(8,128)(2,1)} %attend.1.after_hbm, bf16[16,1024]{1,0:T(8,128)(2,1)S(1)} %copy-done.3, bf16[32,16,256]{2,1,0:T(8,128)(2,1)S(1)} %copy-done, bf16[1024,1024]{1,0:T(8,128)(2,1)S(1)} %copy-done.1, bf16[1024,1024]{1,0:T(8,128)(2,1)S(1)} %copy-done.2), custom_call_target="tpu_custom_call" | custom-call | flops 16777216 | bytes 1048576 | tf_op jit(solution)/shard_map/own/pallas_call | solution.py:443
  40.2 9.1 %all-to-all-done.1.parts_ref = bf16[32,40,128]{2,1,0:T(8,128)(2,1)S(1)} async-done(((bf16[32,40,128]{2,1,0:T(8,128)(2,1)}), bf16[32,40,128]{2,1,0:T(8,128)(2,1)S(1)}, u32[]{:S(2)}, u32[]{:S(2)}) %all-to-all-start.1) | async-done | bytes 327712 | tf_op jit(solution)/shard_map/all_to_all | solution.py:439
  49.2 1.3 %join.1 = bf16[16,256]{1,0:T(8,128)(2,1)} custom-call(bf16[32,40,128]{2,1,0:T(8,128)(2,1)S(1)} %all-to-all-done.1.parts_ref, f32[16,256]{1,0:T(8,128)S(1)} %get-tuple-element.7.self_score_ref, bf16[16,256]{1,0:T(8,128)(2,1)S(1)} %get-tuple-element.8.self_value_ref), custom_call_target="tpu_custom_call" | custom-call | tf_op jit(solution)/shard_map/join/pallas_call | solution.py:466
Async XLA Ops:
  2.3 21.3 %all-to-all-start = ((bf16[32,16,256]{2,1,0:T(8,128)(2,1)}), bf16[32,16,256]{2,1,0:T(8,128)(2,1)S(1)}, u32[]{:S(2)}, u32[]{:S(2)}) async-start(bf16[32,16,256]{2,1,0:T(8,128)(2,1)} %query.1.query_hbm), calls=%async_computation | async-start | bytes 524288 | tf_op jit(solution)/shard_map/all_to_all | solution.py:433
  10.0 13.5 %copy-start.4 = (s32[128]{0:T(128)S(1)}, s32[128]{0:T(128)}, u32[]{:S(2)}) copy-start(s32[128]{0:T(128)} %param.12) | copy-start | bytes 1540
  10.0 13.5 %copy-start.5 = (s32[1,1,16]{2,1,0:T(1,128)S(1)}, s32[1,1,16]{2,1,0:T(1,128)}, u32[]{:S(2)}) copy-start(s32[1,1,16]{2,1,0:T(1,128)} %list_hbm.1) | copy-start | bytes 196
  23.6 14.1 %copy-start = (bf16[32,16,256]{2,1,0:T(8,128)(2,1)S(1)}, bf16[32,16,256]{2,1,0:T(8,128)(2,1)}, u32[]{:S(2)}) copy-start(bf16[32,16,256]{2,1,0:T(8,128)(2,1)} %query.1.query_hbm) | copy-start | bytes 786436
  23.6 14.1 %copy-start.1 = (bf16[1024,1024]{1,0:T(8,128)(2,1)S(1)}, bf16[1024,1024]{1,0:T(8,128)(2,1)}, u32[]{:S(2)}) copy-start(bf16[1024,1024]{1,0:T(8,128)(2,1)} %w_key_hbm.3) | copy-start | bytes 6291460
  23.6 14.1 %copy-start.3 = (bf16[16,1024]{1,0:T(8,128)(2,1)S(1)}, bf16[16,1024]{1,0:T(8,128)(2,1)}, u32[]{:S(2)}) copy-start(bf16[16,1024]{1,0:T(8,128)(2,1)} %latent_ref.1) | copy-start | bytes 98308
  31.8 17.5 %all-to-all-start.1 = ((bf16[32,40,128]{2,1,0:T(8,128)(2,1)}), bf16[32,40,128]{2,1,0:T(8,128)(2,1)S(1)}, u32[]{:S(2)}, u32[]{:S(2)}) async-start(bf16[32,40,128]{2,1,0:T(8,128)(2,1)} %bitcast.2), calls=%async_computation.1 | async-start | bytes 655360 | tf_op jit(solution)/shard_map/all_to_all | solution.py:439
  37.7 1.6 %copy-start.2 = (bf16[1024,1024]{1,0:T(8,128)(2,1)S(1)}, bf16[1024,1024]{1,0:T(8,128)(2,1)}, u32[]{:S(2)}) copy-start(bf16[1024,1024]{1,0:T(8,128)(2,1)} %w_value_hbm.3) | copy-start | bytes 6291460

commit v3 on v2

--- a/solution.py
+++ b/solution.py
@@ -14,7 +14,7 @@
 
 PROJECT_ROWS = 512
 AHEAD = 2
-WEIGHT_PARTS = 1
+WEIGHT_PARTS = 2
 ATTEND_ROWS = 256
 ATTEND_GRANT = 50 * 2**20
 VMEM_GRANT = 12 * 2**20
@@ -46,15 +46,12 @@
     normed = normalize(latent_ref[...])
     weight_copy.wait()
     query = jnp.dot(normed, w_query_ref[...], preferred_element_type=jnp.float32) * HD ** (-0.5)
-    query_ref[...] = query.astype(jnp.bfloat16)
-    copies = [
-        pltpu.make_async_copy(query_ref, out_hbm.at[k], out_sem.at[k])
-        for k in range(out_hbm.shape[0])
-    ]
-    for copy in copies:
-        copy.start()
-    for copy in copies:
-        copy.wait()
+    query = query.astype(jnp.bfloat16)
+    for k in range(out_hbm.shape[0]):
+        query_ref[k] = query
+    out_copy = pltpu.make_async_copy(query_ref, out_hbm, out_sem)
+    out_copy.start()
+    out_copy.wait()
 
 
 def self_kernel(
@@ -103,17 +100,6 @@
             for k in range(WEIGHT_PARTS)
         ]
 
-    def project_rows(normed, ref, waits):
-        parts = []
-        for k in range(WEIGHT_PARTS):
-            if waits:
-                waits[k].wait()
-            part = jnp.dot(
-                normed, ref[:, k * width : (k + 1) * width], preferred_element_type=jnp.float32
-            )
-            parts.append(part.astype(jnp.bfloat16))
-        return jnp.concatenate(parts, axis=1)
-
     first = rows // tile
     key_copies = part_copies(w_key_hbm, w_key_ref, first)
     value_copies = part_copies(w_value_hbm, w_value_ref, first + WEIGHT_PARTS)
@@ -121,26 +107,59 @@
     for copy in key_copies + value_copies + row_copies[1:]:
         copy.start()
     out_copies = []
-    for r in range(0, rows, tile):
+
+    def normed_rows(r):
+        row_copies[r // tile].wait()
+        return normalize(prefix_ref[r : r + tile, :])
+
+    def multiply(normed, ref, copies, k, r):
+        if r == 0:
+            copies[k].wait()
+        part = jnp.dot(
+            normed, ref[:, k * width : (k + 1) * width], preferred_element_type=jnp.float32
+        )
+        return part.astype(jnp.bfloat16)
+
+    def leave(which, r):
         span = pl.ds(r, tile)
-        k = r // tile
-        row_copies[k].wait()
-        normed = normalize(prefix_ref[r : r + tile, :])
-        key = project_rows(normed, w_key_ref, key_copies if r == 0 else None)
-        for p in range(pairs):
-            both_ref[0, p, r : r + tile, :] = key[:, p * PAIR : (p + 1) * PAIR]
-        copy = pltpu.make_async_copy(both_ref.at[0, :, span, :], both_hbm.at[0, :, span, :], out_sem.at[2 * k])
+        copy = pltpu.make_async_copy(
+            both_ref.at[which, :, span, :],
+            both_hbm.at[which, :, span, :],
+            out_sem.at[2 * (r // tile) + which],
+        )
         copy.start()
         out_copies.append(copy)
-        value = project_rows(normed, w_value_ref, value_copies if r == 0 else None)
-        for p in range(pairs):
-            for b in range(r, r + tile, BLOCK):
-                both_ref[1, p, b : b + BLOCK, :] = value[b - r : b - r + BLOCK, p * PAIR : (p + 1) * PAIR].T
-        copy = pltpu.make_async_copy(
-            both_ref.at[1, :, span, :], both_hbm.at[1, :, span, :], out_sem.at[2 * k + 1]
-        )
-        copy.start()
-        out_copies.append(copy)
+
+    def turn(part, k, r):
+        for p in range(width // PAIR):
+            for b in range(0, tile, BLOCK):
+                both_ref[1, k * (width // PAIR) + p, r + b : r + b + BLOCK, :] = part[
+                    b : b + BLOCK, p * PAIR : (p + 1) * PAIR
+                ].T
+
+    waiting = None
+    normed = normed_rows(0)
+    for r in range(0, rows, tile):
+        for k in range(WEIGHT_PARTS):
+            part = multiply(normed, w_key_ref, key_copies, k, r)
+            for p in range(width // PAIR):
+                both_ref[0, k * (width // PAIR) + p, r : r + tile, :] = part[:, p * PAIR : (p + 1) * PAIR]
+            if waiting is not None:
+                turn(*waiting)
+                leave(1, waiting[2])
+                waiting = None
+        leave(0, r)
+        following = None
+        for k in range(WEIGHT_PARTS):
+            part = multiply(normed, w_value_ref, value_copies, k, r)
+            if k == 0 and r + tile < rows:
+                following = normed_rows(r + tile)
+            if waiting is not None:
+                turn(*waiting)
+            waiting = (part, k, r)
+        normed = following
+    turn(*waiting)
+    leave(1, waiting[2])
     for copy in out_copies:
         copy.wait()
 
@@ -228,8 +247,10 @@
     def finish(step, top, sum8, total):
         tile, pair, group, j = place(step)
         sums = jnp.sum(sum8, axis=0, keepdims=True)
-        scaled = total / sums
-        own = jnp.concatenate([scaled[:HD, :LANES], scaled[HD:, LANES:]], axis=0)
+        factor = 1.0 / sums
+        own = jnp.concatenate(
+            [total[:HD, :LANES] * factor[:, :LANES], total[HD:, LANES:] * factor[:, LANES:]], axis=0
+        )
         out_ref[
             pl.ds(tile * ctx_tile, ctx_tile),
             group,
@@ -424,9 +445,9 @@
         scratch_shapes=[
             pltpu.VMEM(latent_inputs.shape, small),
             pltpu.VMEM(w_query.shape, small),
-            pltpu.VMEM((latent_rows, head_width), small),
+            pltpu.VMEM((device_count, latent_rows, head_width), small),
             pltpu.SemaphoreType.DMA((2,)),
-            pltpu.SemaphoreType.DMA((device_count,)),
+            pltpu.SemaphoreType.DMA,
         ],
         name="query",
     )(latent_inputs, w_query)

time: 50.9 us -> 50.1 us (0.984)
  Pallas kernels: 26.2 us -> 25.4 us
where the time goes in v3:
time: 50.1 us; the launch traced here: 49.8 us
  Pallas kernels  25.4 us (51%)
  starting transfers between devices  12.9 us (26%)
  waiting for transfers between devices  9.06 us (18%)
  local copies, waits for them, and re-layouts  1.62 us (3%)
  between operations  0.79 us (2%)
    pallas_call x1, Pallas kernels, project(): pl.pallas_call(functools.partial(project_kernel, tile=PROJECT_ROWS), in_s...  13 us
    all_to_all x1, waiting for transfers between devices, per_device(): lax.all_to_all(packed.reshape(device_count, packed_rows, LANES), axes, sp...  9.06 us
    pallas_call x1, Pallas kernels, attend(): pl.pallas_call(functools.partial(attend_kernel, chunk=ATTEND_ROWS), in_sp...  8.19 us
    all_to_all x1, starting transfers between devices, per_device(): lax.all_to_all(copies, axes, split_axis=0, concat_axis=0, tiled=True)  7.09 us
    all_to_all x1, starting transfers between devices, per_device(): lax.all_to_all(packed.reshape(device_count, packed_rows, LANES), axes, sp...  5.83 us
    pallas_call x1, Pallas kernels, per_device(): pl.pallas_call(query_kernel, in_specs=[HBM] * 2, out_specs=HBM, out_shape...  1.99 us
    unnamed x12, local copies, waits for them, and re-layouts  1.62 us
    pallas_call x1, Pallas kernels, per_device(): pl.pallas_call(join_kernel, in_specs=[VMEM] * 3, out_specs=VMEM, out_shap...  1.32 us
  transfers between devices with their start and end apart: 2, of which 1 were waited for; matrix products, arithmetic and copies ran while one was open for 0% of the time, Pallas kernels for 28%

profile of v3, /device:TPU:1, one launch (start us, length us, event | category | flops | bytes accessed | tf_op | source)
XLA Modules:
  0.0 49.8 jit_solution(9072432495694825770)
XLA Ops:
  0.0 2.0 %query.1.query_hbm = bf16[32,16,256]{2,1,0:T(8,128)(2,1)} custom-call(bf16[16,1024]{1,0:T(8,128)(2,1)} %latent_ref.1, bf16[1024,256]{1,0:T(8,128)(2,1)} %w_query_hbm.1), custom_call_target="tpu_custom_call" | custom-call | tf_op jit(solution)/shard_map/query/pallas_call | solution.py:440
  2.0 7.1 %all-to-all-start = ((bf16[32,16,256]{2,1,0:T(8,128)(2,1)}), bf16[32,16,256]{2,1,0:T(8,128)(2,1)S(1)}, u32[]{:S(2)}, u32[]{:S(2)}) async-start(bf16[32,16,256]{2,1,0:T(8,128)(2,1)} %query.1.query_hbm), calls=%async_computation | async-start | bytes 524288 | tf_op jit(solution)/shard_map/all_to_all | solution.py:454
  9.7 0.0 copy-start.4
  9.8 0.0 copy-start.5
  9.8 13.0 %project.1.both_hbm = bf16[2,8,2048,128]{3,2,1,0:T(8,128)(2,1)} custom-call(bf16[2048,1024]{1,0:T(8,128)(2,1)} %prefix_hbm.1, bf16[1024,1024]{1,0:T(8,128)(2,1)} %w_key_hbm.3, bf16[1024,1024]{1,0:T(8,128)(2,1)} %w_value_hbm.3), custom_call_target="tpu_custom_call" | custom-call | flops 8589934592 | bytes 16777216 | tf_op jit(solution)/shard_map/project/pallas_call | solution.py:332
  22.8 0.0 all-to-all-done
  22.8 0.0 copy-done.4
  22.8 0.0 copy-done.5
  22.8 0.0 copy-start
  22.8 0.0 copy-start.1
  22.8 0.0 copy-start.3
  22.8 8.2 %attend.1.after_hbm = bf16[8,4,40,128]{3,2,1,0:T(8,128)(2,1)} custom-call(s32[1,1]{1,0:T(1,128)S(6)} %copy.9.count_ref, s32[1,128]{1,0:T(1,128)S(1)} %bitcast.4, bf16[8,4,16,256]{3,2,1,0:T(8,128)(2,1)S(1)} %bitcast.3, s32[1,1,16]{2,1,0:T(1,128)S(1)} %copy-done.5, bf16[2,8,2048,128]{3,2,1,0:T(8,128)(2,1)} %project.1.both_hbm), custom_call_target="tpu_custom_call" | custom-call | flops 4294967296 | bytes 8388608 | tf_op jit(solution)/shard_map/attend/pallas_call | solution.py:363
  31.0 5.8 %all-to-all-start.1 = ((bf16[32,40,128]{2,1,0:T(8,128)(2,1)}), bf16[32,40,128]{2,1,0:T(8,128)(2,1)S(1)}, u32[]{:S(2)}, u32[]{:S(2)}) async-start(bf16[32,40,128]{2,1,0:T(8,128)(2,1)} %bitcast.2), calls=%async_computation.1 | async-start | bytes 655360 | tf_op jit(solution)/shard_map/all_to_all | solution.py:460
  36.9 0.0 copy-done
  36.9 0.0 copy-done.1
  36.9 0.0 copy-done.3
  36.9 0.0 copy-start.2
  36.9 1.6 %copy-done.2 = bf16[1024,1024]{1,0:T(8,128)(2,1)S(1)} copy-done((bf16[1024,1024]{1,0:T(8,128)(2,1)S(1)}, bf16[1024,1024]{1,0:T(8,128)(2,1)}, u32[]{:S(2)}) %copy-start.2) | copy-done | bytes 2097176
  38.5 0.9 %own.1 = (f32[16,256]{1,0:T(8,128)S(1)}, bf16[16,256]{1,0:T(8,128)(2,1)S(1)}) custom-call(bf16[8,4,40,128]{3,2,1,0:T(8,128)(2,1)} %attend.1.after_hbm, bf16[16,1024]{1,0:T(8,128)(2,1)S(1)} %copy-done.3, bf16[32,16,256]{2,1,0:T(8,128)(2,1)S(1)} %copy-done, bf16[1024,1024]{1,0:T(8,128)(2,1)S(1)} %copy-done.1, bf16[1024,1024]{1,0:T(8,128)(2,1)S(1)} %copy-done.2), custom_call_target="tpu_custom_call" | custom-call | flops 16777216 | bytes 1048576 | tf_op jit(solution)/shard_map/own/pallas_call | solution.py:464
  39.4 9.1 %all-to-all-done.1.parts_ref = bf16[32,40,128]{2,1,0:T(8,128)(2,1)S(1)} async-done(((bf16[32,40,128]{2,1,0:T(8,128)(2,1)}), bf16[32,40,128]{2,1,0:T(8,128)(2,1)S(1)}, u32[]{:S(2)}, u32[]{:S(2)}) %all-to-all-start.1) | async-done | bytes 327712 | tf_op jit(solution)/shard_map/all_to_all | solution.py:460
  48.5 1.3 %join.1 = bf16[16,256]{1,0:T(8,128)(2,1)} custom-call(bf16[32,40,128]{2,1,0:T(8,128)(2,1)S(1)} %all-to-all-done.1.parts_ref, f32[16,256]{1,0:T(8,128)S(1)} %get-tuple-element.7.self_score_ref, bf16[16,256]{1,0:T(8,128)(2,1)S(1)} %get-tuple-element.8.self_value_ref), custom_call_target="tpu_custom_call" | custom-call | tf_op jit(solution)/shard_map/join/pallas_call | solution.py:487
Async XLA Ops:
  2.0 20.8 %all-to-all-start = ((bf16[32,16,256]{2,1,0:T(8,128)(2,1)}), bf16[32,16,256]{2,1,0:T(8,128)(2,1)S(1)}, u32[]{:S(2)}, u32[]{:S(2)}) async-start(bf16[32,16,256]{2,1,0:T(8,128)(2,1)} %query.1.query_hbm), calls=%async_computation | async-start | bytes 524288 | tf_op jit(solution)/shard_map/all_to_all | solution.py:454
  9.7 13.1 %copy-start.4 = (s32[128]{0:T(128)S(1)}, s32[128]{0:T(128)}, u32[]{:S(2)}) copy-start(s32[128]{0:T(128)} %param.12) | copy-start | bytes 1540
  9.8 13.1 %copy-start.5 = (s32[1,1,16]{2,1,0:T(1,128)S(1)}, s32[1,1,16]{2,1,0:T(1,128)}, u32[]{:S(2)}) copy-start(s32[1,1,16]{2,1,0:T(1,128)} %list_hbm.1) | copy-start | bytes 196
  22.8 14.1 %copy-start = (bf16[32,16,256]{2,1,0:T(8,128)(2,1)S(1)}, bf16[32,16,256]{2,1,0:T(8,128)(2,1)}, u32[]{:S(2)}) copy-start(bf16[32,16,256]{2,1,0:T(8,128)(2,1)} %query.1.query_hbm) | copy-start | bytes 786436
  22.8 14.1 %copy-start.1 = (bf16[1024,1024]{1,0:T(8,128)(2,1)S(1)}, bf16[1024,1024]{1,0:T(8,128)(2,1)}, u32[]{:S(2)}) copy-start(bf16[1024,1024]{1,0:T(8,128)(2,1)} %w_key_hbm.3) | copy-start | bytes 6291460
  22.8 14.1 %copy-start.3 = (bf16[16,1024]{1,0:T(8,128)(2,1)S(1)}, bf16[16,1024]{1,0:T(8,128)(2,1)}, u32[]{:S(2)}) copy-start(bf16[16,1024]{1,0:T(8,128)(2,1)} %latent_ref.1) | copy-start | bytes 98308
  31.0 17.5 %all-to-all-start.1 = ((bf16[32,40,128]{2,1,0:T(8,128)(2,1)}), bf16[32,40,128]{2,1,0:T(8,128)(2,1)S(1)}, u32[]{:S(2)}, u32[]{:S(2)}) async-start(bf16[32,40,128]{2,1,0:T(8,128)(2,1)} %bitcast.2), calls=%async_computation.1 | async-start | bytes 655360 | tf_op jit(solution)/shard_map/all_to_all | solution.py:460
  36.9 1.6 %copy-start.2 = (bf16[1024,1024]{1,0:T(8,128)(2,1)S(1)}, bf16[1024,1024]{1,0:T(8,128)(2,1)}, u32[]{:S(2)}) copy-start(bf16[1024,1024]{1,0:T(8,128)(2,1)} %w_value_hbm.3) | copy-start | bytes 6291460
